TPU v7x, 128 devices: a whole 4x4x4 slice. The times are simulated.
128 devices in a mesh: dp: 4 (over y), vocab: 32 (over z, x, core).
Axes of the slice: x: 4, y: 4, z: 4, core: 2. Of those that a mesh axis runs over, the one named last changes fastest.
Arguments:
- input_ids: int32 [1024], P('dp'), may hold values from 0 to 255999
- target_ids: int32 [1024], P('dp'), may hold values from 0 to 255999
- loss_mask: int32 [1024], P('dp'), may hold values 0 or 1
- final_hidden: bfloat16 [1024, 3584], P('dp'), may hold values from -5 to 5, as said below
- norm_gain: float32 [3584], replicated, may hold values from 0.25 to 1.75
- embed_cotangent: bfloat16 [1024, 3584], P('dp'), may hold values from -0.059814453 to 0.059814453
- table: bfloat16 [256000, 3584], P(('dp', 'vocab')), may hold values from -0.08351914 to 0.08351914, as said below
Outputs:
- embedded: bfloat16 [1024, 3584], P('dp')
- loss: float32 [], replicated
- grad_hidden: bfloat16 [1024, 3584], P('dp')
- gain_grad: float32 [3584], replicated
- table_grad: bfloat16 [256000, 3584], P(('dp', 'vocab'))
Inputs may be any that keep to these rules, and one draw needn't show every extreme that they name: Every entry of table lies within -5 / sqrt(3584) and 5 / sqrt(3584). Every entry of final_hidden lies within -5 and 5.
All inputs are finite; a program needn't handle non-finite values.
Results may differ from a plain program's by a relative error of at most 0.003.
Values may be sent and summed in bfloat16 or wider, within the bound.
A program may use at most 256 MiB of HBM per device.

v0:
```python
import functools
import math

import jax
import jax.numpy as jnp
from jax import lax
from jax.experimental import pallas as pl
from jax.experimental.pallas import tpu as pltpu
from jax.sharding import PartitionSpec as P

SOFTCAP = 30
EPSILON = 1e-06
LANES = 128


def enter(count, others):
    barrier = pltpu.get_barrier_semaphore()
    for other in others:
        pl.semaphore_signal(barrier, inc=1, device_id={"vocab": other})
    pl.semaphore_wait(barrier, count)


def stats_kernel(n, x_ref, out_ref, slots, mine, send_sem, recv_sem):
    me = lax.axis_index("vocab")
    enter(n - 1, [lax.rem(me + o, n) for o in range(1, n)])
    mine[...] = x_ref[...]

    def copy(o):
        return pltpu.make_async_remote_copy(
            src_ref=mine,
            dst_ref=slots.at[me],
            send_sem=send_sem.at[o],
            recv_sem=recv_sem.at[o],
            device_id={"vocab": lax.rem(me + o, n)},
        )

    def arrival(o):
        return pltpu.make_async_remote_copy(
            src_ref=mine,
            dst_ref=slots.at[lax.rem(me - o + n, n)],
            send_sem=send_sem.at[o],
            recv_sem=recv_sem.at[o],
            device_id={"vocab": lax.rem(me + o, n)},
        )

    for o in range(1, n):
        copy(o).start()
    slots[me] = x_ref[...]
    for o in range(1, n):
        arrival(o).wait_recv()
    total = slots[0]
    for source in range(1, n):
        total = total + slots[source]
    out_ref[...] = total
    for o in range(1, n):
        copy(o).wait_send()


def exchange_stats(n, values):
    if n == 1:
        return values
    return pl.pallas_call(
        functools.partial(stats_kernel, n),
        out_shape=jax.ShapeDtypeStruct(values.shape, values.dtype),
        in_specs=[pl.BlockSpec(memory_space=pltpu.VMEM)],
        out_specs=pl.BlockSpec(memory_space=pltpu.VMEM),
        scratch_shapes=[
            pltpu.VMEM((n,) + values.shape, values.dtype),
            pltpu.VMEM(values.shape, values.dtype),
            pltpu.SemaphoreType.DMA((n,)),
            pltpu.SemaphoreType.DMA((n,)),
        ],
        compiler_params=pltpu.CompilerParams(collective_id=1, has_side_effects=True),
        cost_estimate=pl.CostEstimate(flops=0, bytes_accessed=2**25, transcendentals=0),
    )(values)


def stream_plan(levels, width):
    rest = [g for g in ([1], [2], list(range(3, levels))) if g and g[-1] < levels]
    shares = [11, 10, 7]
    tiles = width // LANES
    plans, start = [], 0
    for i in range(max(1, len(rest))):
        order = [0] + [b for g in rest[i:] + rest[:i] for b in g]
        last = i == max(1, len(rest)) - 1
        stop = tiles if last else start + tiles * shares[i] // sum(shares)
        plans.append((slice(start * LANES, stop * LANES), order))
        start = stop
    return plans


def hidden_kernel(levels, plans, *refs):
    count = len(plans)
    up_ref, found_ref, hidden_ref, gain_ref, grad_ref, emb_ref, gain_out_ref = refs[:7]
    scratch = list(refs[7:])
    acc = [scratch.pop(0) for _ in plans]
    got_wide = [scratch.pop(0) for _ in plans]
    low = [scratch.pop(0) for _ in plans]
    got = [scratch.pop(0) for _ in plans]
    whole = [scratch.pop(0) for _ in plans]
    fwhole = [scratch.pop(0) for _ in plans]
    gains, gain_got, send_sem, recv_sem = scratch
    n = 2**levels
    width = up_ref.shape[2]
    me = lax.axis_index("vocab")
    bits = [lax.rem(me // 2**b, 2) for b in range(levels)]
    partner = [me + (1 - 2 * bits[b]) * 2**b for b in range(levels)]
    enter(levels, partner)

    def chunk_of(position, order):
        return sum(
            lax.rem(position // 2 ** (levels - 1 - j), 2) * 2 ** order[j] for j in range(levels)
        )

    def base_of(order, known):
        return sum([bits[order[j]] * 2 ** (levels - 1 - j) for j in range(known)], 0)

    def each(size, step):
        def wrapped(i, carry):
            step(i)
            return carry

        lax.fori_loop(0, size, wrapped, 0, unroll=min(size, 4))

    def remote(src, dst, flow, stage, bit):
        return pltpu.make_async_remote_copy(
            src_ref=src,
            dst_ref=dst,
            send_sem=send_sem.at[flow, stage],
            recv_sem=recv_sem.at[flow, stage],
            device_id={"vocab": partner[bit]},
        )

    def gather_copy(buffers, flow, s, t):
        order = plans[s][1]
        block = pl.ds(base_of(order, levels - t), 2**t)
        bit = order[levels - 1 - t]
        stage = levels + t
        return remote(buffers[s].at[block], buffers[s].at[block], flow + s, stage, bit)

    for s, (columns, order) in enumerate(plans):
        fwhole[s][base_of(order, levels)] = found_ref[:, columns].astype(jnp.bfloat16)

    for k in range(levels):
        size = 2 ** (levels - 1 - k)
        wide = k not in (1, 2)
        sent, landed = (acc, got_wide) if wide else (low, got)
        copies = []
        for s, (columns, order) in enumerate(plans):
            bit = order[k]
            base = base_of(order, k)
            keep = base + bits[bit] * size
            give = base + (1 - bits[bit]) * size

            def prepare(i, s=s, order=order, columns=columns, give=give, keep=keep):
                if k == 0:
                    out_chunk = chunk_of(give + i, order)
                    acc[s][give + i] = up_ref[out_chunk, :, columns]
                elif not wide:
                    low[s][give + i] = acc[s][give + i].astype(jnp.bfloat16)

            each(size, prepare)
            arrived = pl.ds(size, size)
            first = remote(
                sent[s].at[pl.ds(give, size)], landed[s].at[arrived], s, k, bit
            )
            first.start()
            second = gather_copy(fwhole, count, s, k)
            second.start()
            copies.append((first, second, keep))
        for s, (columns, order) in enumerate(plans):
            first, second, keep = copies[s]
            first.wait_recv()

            def add(i, s=s, order=order, columns=columns, keep=keep, landed=landed):
                arrived = landed[s][size + i].astype(jnp.float32)
                if k == 0:
                    acc[s][keep + i] = up_ref[chunk_of(keep + i, order), :, columns] + arrived
                else:
                    acc[s][keep + i] = acc[s][keep + i] + arrived

            each(size, add)
            second.wait_recv()
        for first, second, _ in copies:
            first.wait_send()
            second.wait_send()

    full = hidden_ref[...]
    inv = lax.rsqrt(jnp.sum(full * full, axis=1, keepdims=True) / width + EPSILON)
    own = [base_of(order, levels) for _, order in plans]
    dot = sum(
        jnp.sum(
            acc[s][own[s]] * gain_ref[:, columns] * full[:, columns], axis=1, keepdims=True
        )
        for s, (columns, _) in enumerate(plans)
    )
    mean_dot = dot / width
    gains[0] = jnp.zeros(gains.shape[1:], jnp.float32)
    for s, (columns, _) in enumerate(plans):
        upstream = acc[s][own[s]]
        wide = full[:, columns]
        gradient = inv * (upstream * gain_ref[:, columns]) - wide * (inv * inv * inv) * mean_dot
        whole[s][own[s]] = gradient.astype(jnp.bfloat16)
        part = jnp.sum(upstream * wide * inv, axis=0, keepdims=True)
        for j in range(columns.start // LANES, columns.stop // LANES):
            lanes = slice(j * LANES - columns.start, (j + 1) * LANES - columns.start)
            gains[0, j : j + 1, :] = part[:, lanes]

    for t in range(levels):
        copies = [gather_copy(whole, 0, s, t) for s in range(count)]
        copies.append(remote(gains.at[t], gain_got.at[t], 2 * count, levels + t, t))
        for copy in copies:
            copy.start()
        for copy in copies:
            copy.wait_recv()
        gains[t + 1] = gains[t] + gain_got[t]
        for copy in copies:
            copy.wait_send()
    gain_out_ref[...] = gains[levels]
    for s, (columns, order) in enumerate(plans):

        def place(i, s=s, order=order, columns=columns):
            pair = chunk_of(i, order) // 2
            for out_ref, source in ((grad_ref, whole[s]), (emb_ref, fwhole[s])):
                both = [source[p].astype(jnp.float32) for p in (i, i + n // 2)]
                out_ref[pair, :, columns] = jnp.concatenate(both, axis=0).astype(jnp.bfloat16)

        each(n // 2, place)


def reduce_hidden(n, upstream, found, final_hidden, norm_gain):
    tokens, width = upstream.shape
    levels = n.bit_length() - 1
    share = tokens // n
    plans = stream_plan(levels, width)
    sizes = [(n, share, columns.stop - columns.start) for columns, _ in plans]
    narrow = [pltpu.VMEM((n + 1,) + size[1:], jnp.bfloat16) for size in sizes]
    first = lax.axis_index("vocab") * share
    own_hidden = lax.dynamic_slice_in_dim(final_hidden, first, share, 0).astype(jnp.float32)
    lines = -(-width // (8 * LANES)) * 8
    pairs = (n // 2, 2 * share, width)
    blocks = (n, share, width)
    flows = 2 * len(plans) + 1
    vmem = pl.BlockSpec(memory_space=pltpu.VMEM)
    grad, emb, gain = pl.pallas_call(
        functools.partial(hidden_kernel, levels, plans),
        out_shape=(
            jax.ShapeDtypeStruct(pairs, jnp.bfloat16),
            jax.ShapeDtypeStruct(pairs, jnp.bfloat16),
            jax.ShapeDtypeStruct((lines, LANES), jnp.float32),
        ),
        in_specs=[vmem] * 4,
        out_specs=(vmem, vmem, vmem),
        scratch_shapes=[pltpu.VMEM(size, jnp.float32) for size in sizes] * 2
        + narrow * 4
        + [
            pltpu.VMEM((levels + 1, lines, LANES), jnp.float32),
            pltpu.VMEM((levels, lines, LANES), jnp.float32),
            pltpu.SemaphoreType.DMA((flows, 2 * levels)),
            pltpu.SemaphoreType.DMA((flows, 2 * levels)),
        ],
        compiler_params=pltpu.CompilerParams(
            collective_id=2, has_side_effects=True, vmem_limit_bytes=48 * 1024 * 1024
        ),
    )(
        upstream.reshape(blocks),
        found,
        own_hidden,
        jnp.broadcast_to(norm_gain, (share, width)),
    )
    return grad.reshape(tokens, width), emb.reshape(tokens, width), gain.reshape(-1)[:width]


def halving_sum(n, values):
    me = lax.axis_index("vocab")
    for b in range(n.bit_length() - 1):
        bit = lax.rem(me // 2**b, 2)
        half = values.shape[0] // 2
        give = lax.dynamic_slice_in_dim(values, (1 - bit) * half, half, 0)
        keep = lax.dynamic_slice_in_dim(values, bit * half, half, 0)
        pairs = [(d, d ^ 2**b) for d in range(n)]
        arrived = lax.ppermute(give.astype(jnp.bfloat16), "vocab", pairs)
        values = keep.astype(jnp.float32) + arrived.astype(jnp.float32)
    return values


def reversed_bits(n, values):
    levels = n.bit_length() - 1
    split = values.reshape((2,) * levels + (values.shape[0] // n,))
    return split.transpose(tuple(reversed(range(levels))) + (levels,)).reshape(values.shape)


def table_kernel(scale, step, ids_ref, slope_ref, normed_ref, cotangent_ref, out_ref):
    rows, tokens = slope_ref.shape
    row_ids = lax.broadcasted_iota(jnp.int32, (rows, tokens), 0) + pl.program_id(0) * rows
    hit = (row_ids == ids_ref[...]).astype(jnp.float32).astype(jnp.bfloat16)

    def tile(j, carry):
        columns = pl.ds(pl.multiple_of(j * step, step), step)
        head = jnp.dot(
            slope_ref[...], normed_ref[:, columns], preferred_element_type=jnp.float32
        )
        embed = jnp.dot(hit, cotangent_ref[:, columns], preferred_element_type=jnp.float32)
        out_ref[:, columns] = (head + embed * scale).astype(jnp.bfloat16)
        return carry

    lax.fori_loop(0, out_ref.shape[1] // step, tile, 0)


def table_gradient(scale, local_ids, slope, normed, cotangent):
    row_count, tokens = slope.shape
    width = normed.shape[1]
    block = max(b for b in range(16, 401, 16) if row_count % b == 0)
    step = 512 if width % 512 == 0 else LANES
    vmem = pl.BlockSpec(memory_space=pltpu.VMEM)
    return pl.pallas_call(
        functools.partial(table_kernel, scale, step),
        grid=(row_count // block,),
        out_shape=jax.ShapeDtypeStruct((row_count, width), jnp.bfloat16),
        in_specs=[vmem, pl.BlockSpec((block, tokens), lambda i: (i, 0)), vmem, vmem],
        out_specs=pl.BlockSpec((block, width), lambda i: (i, 0)),
        compiler_params=pltpu.CompilerParams(vmem_limit_bytes=48 * 1024 * 1024),
        cost_estimate=pl.CostEstimate(
            flops=4 * row_count * tokens * width,
            bytes_accessed=2 * row_count * width,
            transcendentals=0,
        ),
    )(local_ids.reshape(1, tokens), slope, normed, cotangent)


def body(input_ids, target_ids, loss_mask, final_hidden, norm_gain, embed_cotangent, table):
    row_count, width = table.shape
    embed_scale = math.sqrt(width)
    n = lax.axis_size("vocab")
    first_row = lax.axis_index(("dp", "vocab")) * row_count
    every_id, every_target, every_mask = (
        lax.all_gather(a, "dp", axis=0, tiled=True) for a in (input_ids, target_ids, loss_mask)
    )
    tokens = every_id.shape[0]
    widened = final_hidden.astype(jnp.float32)
    inv_rms = lax.rsqrt(jnp.mean(widened * widened, axis=1, keepdims=True) + EPSILON)
    normed = (widened * inv_rms * norm_gain).astype(jnp.bfloat16)
    normed_all, cotangent_all = (
        lax.all_gather(a, "dp", axis=0, tiled=True) for a in (normed, embed_cotangent)
    )
    share = tokens // lax.axis_size("dp") // n
    groups = every_id.reshape(-1, n * share)
    sorted_id = jax.vmap(functools.partial(reversed_bits, n))(groups).reshape(-1)
    id_rows = lax.broadcasted_iota(jnp.int32, (tokens, row_count), 1) + first_row
    id_hit = lax.optimization_barrier((id_rows == sorted_id[:, None]).astype(jnp.bfloat16))
    found = lax.dot_general(
        id_hit, table, (((1,), (0,)), ((), ())), preferred_element_type=jnp.float32
    ).astype(jnp.bfloat16)
    if lax.axis_size("dp") > 1:
        found = lax.psum_scatter(found, "dp", scatter_dimension=0, tiled=True)
    found = halving_sum(n, found)
    raw_logits = lax.dot_general(
        table, normed_all, (((1,), (1,)), ((), ())), preferred_element_type=jnp.float32
    )
    capped = SOFTCAP * jnp.tanh(raw_logits / SOFTCAP)
    row_ids = lax.broadcasted_iota(jnp.int32, capped.shape, 0) + first_row
    target_hit = row_ids == every_target[None, :]
    token_weight = every_mask.astype(jnp.float32)
    sums = jnp.stack(
        [jnp.sum(jnp.exp(capped), axis=0), jnp.sum(jnp.where(target_hit, capped, 0.0), axis=0)]
    )
    sums = exchange_stats(n, sums.reshape(-1, LANES)).reshape(2, tokens)
    sum_exp, target_logit = lax.psum(sums, "dp")
    loss = jnp.sum(token_weight * (jnp.log(sum_exp) - target_logit)) / jnp.maximum(
        jnp.sum(token_weight), 1.0
    )
    slope = (
        token_weight[None, :]
        * (jnp.exp(capped) / sum_exp[None, :] - target_hit.astype(jnp.float32))
        * (1.0 - (capped / SOFTCAP) ** 2)
    ).astype(jnp.bfloat16)
    slope = lax.optimization_barrier(slope)
    upstream = lax.dot_general(
        slope, table, (((0,), (0,)), ((), ())), preferred_element_type=jnp.float32
    )
    if lax.axis_size("dp") > 1:
        upstream = lax.psum_scatter(upstream, "dp", scatter_dimension=0, tiled=True)
    grad_hidden, rows, gain_part = reduce_hidden(n, upstream, found, final_hidden, norm_gain)
    embedded = (rows.astype(jnp.float32) * embed_scale).astype(jnp.bfloat16)
    gain_grad = lax.psum(gain_part, "dp")
    table_grad = table_gradient(
        embed_scale, every_id - first_row, slope, normed_all, cotangent_all
    )
    return (embedded, loss, grad_hidden, gain_grad, table_grad)


def solution(mesh):
    placed = (
        P("dp"),
        P("dp"),
        P("dp"),
        P("dp", None),
        P(),
        P("dp", None),
        P(("dp", "vocab"), None),
    )
    return jax.shard_map(
        body,
        mesh=mesh,
        in_specs=placed,
        out_specs=(P("dp", None), P(), P("dp", None), P(), P(("dp", "vocab"), None)),
        check_vma=False,
    )
```

profile of v0, /device:TPU:0, one launch (start us, length us, event | category | flops | bytes accessed | tf_op | source)
XLA Modules:
  0.0 473.4 jit_solution(15421801653486595925)
XLA Ops:
  7.2 0.0 all-gather.6.cloned.1.call-start
  7.2 1.9 fusion.6
  9.2 3.2 fusion.8
  12.4 0.0 reduce-scatter.5.cloned.1.call-start
  12.5 10.1 %all-gather.2 = s32[4,1,256]{2,1,0:T(1,128)S(1)} all-gather(s32[1,1,256]{2,1,0:T(1,128)S(1)} %bitcast.45), channel_id=1, replica_groups=mesh['dp'=4,'vocab'=32] {'dp'}, dimensions={0}, use_global_device_ids=true | all-gather | bytes 5120 | tf_op jit(solution)/shard_map/all_gather | solution.py:337
  22.7 0.2 reshape_reshape.3
  22.9 0.1 eq.20
  23.0 0.8 compare_convert_fusion.1
  23.8 20.4 %convolution_convert_fusion = bf16[1024,3584]{1,0:T(8,128)(2,1)} fusion(bf16[1024,2000]{1,0:T(8,128)(2,1)S(1)} %compare_convert_fusion.1, bf16[2000,3584]{1,0:T(8,128)(2,1)} %param.13), kind=kOutput, calls=%fused_computation.11 | convolution fusion | flops 14683734016 | bytes 25772032 | tf_op jit(solution)/shard_map/dot_general | solution.py:351
  44.2 0.0 all-gather.8.cloned.1.call-start
  44.3 0.7 all-gather.8.cloned.1.call-update
  45.0 0.0 reduce-scatter.3.cloned.1.call-start
  45.0 7.1 %all-gather = s32[4,1,256]{2,1,0:T(1,128)S(1)} all-gather(s32[1,1,256]{2,1,0:T(1,128)S(1)} %bitcast.46), channel_id=1, replica_groups=mesh['dp'=4,'vocab'=32] {'dp'}, dimensions={0}, use_global_device_ids=true | all-gather | bytes 5120 | tf_op jit(solution)/shard_map/all_gather | solution.py:337
  52.1 9.1 %all-gather.1 = s32[4,1,256]{2,1,0:T(1,128)S(1)} all-gather(s32[1,1,256]{2,1,0:T(1,128)S(1)} %bitcast.47), channel_id=1, replica_groups=mesh['dp'=4,'vocab'=32] {'dp'}, dimensions={0}, use_global_device_ids=true | all-gather | bytes 5120 | tf_op jit(solution)/shard_map/all_gather | solution.py:337
  61.1 28.4 %all-gather.6.cloned.1.call-done.normed_ref = bf16[1024,3584]{1,0:T(8,128)(2,1)} async-done(((bf16[256,3584]{1,0:T(8,128)(2,1)}), bf16[1024,3584]{1,0:T(8,128)(2,1)}) %all-gather.6.cloned.1.call-update) | async-done | bytes 7340048 | tf_op jit(solution)/shard_map/all_gather | solution.py:344
  89.5 23.0 %fusion.5 = (f32[1024]{0:T(1024)S(1)}, f32[1024]{0:T(1024)S(1)}, f32[1024,2000]{0,1:T(8,128)}) fusion(s32[1024]{0:T(1024)S(1)} %bitcast.40, s32[2000]{0:T(1024)S(1)} %iota_add_fusion, bf16[1024,3584]{1,0:T(8,128)(2,1)} %all-gather.6.cloned.1.call-done.normed_ref, bf16[2000,3584]{1,0:T(8,128)(2,1)} %param.13), kind=kOutput, calls=%fused_computation.10 | convolution fusion | flops 14692349952 | bytes 29888320 | tf_op jit(solution)/shard_map/dot_general | solution.py:357
  112.5 0.6 reshape.45.x_ref
  113.1 12.4 %shard_map.110 = f32[16,128]{1,0:T(8,128)} custom-call(f32[16,128]{1,0:T(8,128)} %reshape.45.x_ref), custom_call_target="tpu_custom_call" | custom-call | bytes 33554432 | tf_op jit(solution)/shard_map/pallas_call | solution.py:62
  125.5 0.7 reshape.46
  126.3 9.8 %psum.14 = f32[2,1024]{1,0:T(2,128)S(1)} all-reduce(f32[2,1024]{1,0:T(2,128)S(1)} %reshape.46), channel_id=1, replica_groups=mesh['dp'=4,'vocab'=32] {'dp'}, use_global_device_ids=true, to_apply=%region_3.4 | all-reduce | flops 2048 | bytes 16384 | tf_op jit(solution)/shard_map/psum | solution.py:368
  136.1 6.4 %fusion.4.slope_ref = bf16[2000,1024]{1,0:T(8,128)(2,1)S(1)} fusion(f32[1024,2000]{0,1:T(8,128)} %get-tuple-element.17, f32[1024]{0:T(1024)S(1)} %bitcast.38, s32[1024]{0:T(1024)S(1)} %bitcast.41, f32[1024]{0:T(1024)S(1)} %bitcast.36, s32[2000]{0:T(1024)S(1)} %iota_add_fusion), kind=kLoop, calls=%fused_computation.7 | loop fusion | flops 22528000 | bytes 12308288 | tf_op jit(solution)/shard_map/convert_element_type | solution.py:376
  142.6 22.3 %fusion.10 = f32[1024,3584]{1,0:T(8,128)} fusion(bf16[2000,1024]{1,0:T(8,128)(2,1)S(1)} %fusion.4.slope_ref, bf16[2000,3584]{1,0:T(8,128)(2,1)} %param.13), kind=kOutput, calls=%fused_computation.37 | convolution fusion | flops 14680064000 | bytes 33112064 | tf_op jit(solution)/shard_map/dot_general | solution.py:378
  164.8 2.0 copy-done
  166.8 0.0 reduce-scatter.5.cloned.1.call-done
  166.9 1.2 constant_dynamic-slice_fusion
  168.1 0.1 collective-permute-start
  168.2 2.4 collective-permute-done
  170.7 1.4 convert_add_fusion
  172.1 0.1 dynamic-slice_convert_fusion
  172.2 1.1 collective-permute-start.1
  173.3 0.6 convert_reduce_fusion
  174.5 10.3 %collective-permute-done.1 = bf16[64,3584]{1,0:T(8,128)(2,1)S(1)} collective-permute-done((bf16[64,3584]{1,0:T(8,128)(2,1)S(1)}, bf16[64,3584]{1,0:T(8,128)(2,1)S(1)}, u32[]{:S(2)}, u32[]{:S(2)}) %collective-permute-start.1) | collective-permute-done | bytes 458784 | tf_op jit(solution)/shard_map/ppermute | solution.py:282
  184.8 0.1 convert_add_fusion.1
  185.0 2.8 collective-permute-start.2
  187.8 0.8 dynamic-slice_convert_fusion.4.refs_2_
  188.6 5.2 %collective-permute-done.2 = bf16[32,3584]{1,0:T(8,128)(2,1)S(1)} collective-permute-done((bf16[32,3584]{1,0:T(8,128)(2,1)S(1)}, bf16[32,3584]{1,0:T(8,128)(2,1)S(1)}, u32[]{:S(2)}, u32[]{:S(2)}) %collective-permute-start.2) | collective-permute-done | bytes 229408 | tf_op jit(solution)/shard_map/ppermute | solution.py:282
  193.8 1.1 collective-permute-start.3
  195.0 46.1 %all-gather.8.cloned.1.call-done.cotangent_ref = bf16[1024,3584]{1,0:T(8,128)(2,1)} async-done(((bf16[256,3584]{1,0:T(8,128)(2,1)}), bf16[1024,3584]{1,0:T(8,128)(2,1)}) %all-gather.8.cloned.1.call-update) | async-done | bytes 7340048 | tf_op jit(solution)/shard_map/all_gather | solution.py:344
  241.1 2.2 copy-done.1
  243.3 42.9 %shard_map.112 = bf16[2000,3584]{1,0:T(8,128)(2,1)} custom-call(s32[1,1024]{1,0:T(1,128)S(1)} %bitcast.32, bf16[2000,1024]{1,0:T(8,128)(2,1)S(1)} %copy-done.1, bf16[1024,3584]{1,0:T(8,128)(2,1)} %all-gather.6.cloned.1.call-done.normed_ref, bf16[1024,3584]{1,0:T(8,128)(2,1)} %all-gather.8.cloned.1.call-done.cotangent_ref), custom_call_target="tpu_custom_call" | custom-call | flops 29360128000 | bytes 14336000 | tf_op jit(solution)/shard_map/pallas_call | solution.py:316
  286.2 3.2 collective-permute-start.4
  289.4 0.6 multiply_reduce_fusion
  290.7 1.3 collective-permute-done.4
  292.0 83.8 %reduce-scatter.3.cloned.1.call-done = f32[256,3584]{1,0:T(8,128)} async-done(((f32[1024,3584]{1,0:T(8,128)}), f32[256,3584]{1,0:T(8,128)}) %reduce-scatter.3.cloned.1.call-update) | async-done | bytes 3670032 | tf_op jit(solution)/shard_map/reduce_scatter | solution.py:382
  375.8 71.6 %shard_map.111 = (bf16[16,16,3584]{2,1,0:T(8,128)(2,1)S(1)}, bf16[16,16,3584]{2,1,0:T(8,128)(2,1)S(1)}, f32[32,128]{1,0:T(8,128)S(1)}) custom-call(f32[32,8,3584]{2,1,0:T(8,128)} %bitcast.33, f32[8,3584]{1,0:T(8,128)S(1)} %convert_add_fusion.4.refs_1_, f32[8,3584]{1,0:T(8,128)S(1)} %dynamic-slice_convert_fusion.4.refs_2_, f32[8,3584]{1,0:T(8,128)S(1)} %broadcast_in_dim.12.refs_3_), custom_call_target="tpu_custom_call" | custom-call | tf_op jit(solution)/shard_map/pallas_call | solution.py:245
  447.4 1.6 multiply_convert_fusion
  449.0 15.6 %psum.15 = f32[3584]{0:T(1024)} all-reduce(f32[3584]{0:T(1024)S(1)} %slice_bitcast_fusion), channel_id=1, replica_groups=mesh['dp'=4,'vocab'=32] {'dp'}, use_global_device_ids=true, to_apply=%region_8.9 | all-reduce | flops 3584 | bytes 28672 | tf_op jit(solution)/shard_map/psum | solution.py:385
  464.5 1.2 copy.15
  (29 shorter events, 0.3 us)
Async XLA Ops:
  7.2 5.3 %copy-start.3 = (s32[256]{0:T(256)S(1)}, s32[256]{0:T(256)}, u32[]{:S(2)}) copy-start(s32[256]{0:T(256)} %param.7) | copy-start | bytes 3076
  7.2 82.3 %all-gather.6.cloned.1.call-start = ((), (), s32[]{:S(2)}) async-start(), calls=%async_computation.2 | async-start | bytes 9175040 | tf_op jit(solution)/shard_map/all_gather | solution.py:344
  12.4 154.4 %reduce-scatter.5.cloned.1.call-start = ((), (), s32[]{:S(2)}) async-start(), calls=%async_computation.4 | async-start | bytes 9175040 | tf_op jit(solution)/shard_map/reduce_scatter | solution.py:355
  44.2 0.8 copy-start.4
  44.2 7.9 %copy-start.5 = (s32[256]{0:T(256)S(1)}, s32[256]{0:T(256)}, u32[]{:S(2)}) copy-start(s32[256]{0:T(256)} %param.8) | copy-start | bytes 3076
  44.2 196.9 %all-gather.8.cloned.1.call-start = ((), (), s32[]{:S(2)}) async-start(), calls=%async_computation.5 | async-start | bytes 9175040 | tf_op jit(solution)/shard_map/all_gather | solution.py:344
  45.0 330.8 %reduce-scatter.3.cloned.1.call-start = ((), (), s32[]{:S(2)}) async-start(), calls=%async_computation.3 | async-start | bytes 18350080 | tf_op jit(solution)/shard_map/reduce_scatter | solution.py:382
  164.8 2.0 copy-start
  168.1 2.6 collective-permute-start
  172.2 12.6 %collective-permute-start.1 = (bf16[64,3584]{1,0:T(8,128)(2,1)S(1)}, bf16[64,3584]{1,0:T(8,128)(2,1)S(1)}, u32[]{:S(2)}, u32[]{:S(2)}) collective-permute-start(bf16[64,3584]{1,0:T(8,128)(2,1)S(1)} %dynamic-slice_convert_fusion), channel_id=1, source_target_pairs={{0,2},{1,3},{2,0},{3,1},{4,6},{5,7},{6,4},{7,5},{8,10},{9,11},{10,... | collective-permute-start | bytes 1376264 | tf_op jit(solution)/shard_map/ppermute | solution.py:282
  185.0 8.8 %collective-permute-start.2 = (bf16[32,3584]{1,0:T(8,128)(2,1)S(1)}, bf16[32,3584]{1,0:T(8,128)(2,1)S(1)}, u32[]{:S(2)}, u32[]{:S(2)}) collective-permute-start(bf16[32,3584]{1,0:T(8,128)(2,1)S(1)} %dynamic-slice_convert_fusion.1), channel_id=1, source_target_pairs={{0,4},{1,5},{2,6},{3,7},{4,0},{5,1},{6,2},{7,3},{8,12},{9,13},{10,... | collective-permute-start | bytes 688136 | tf_op jit(solution)/shard_map/ppermute | solution.py:282
  193.8 92.3 %collective-permute-start.3 = (bf16[16,3584]{1,0:T(8,128)(2,1)S(1)}, bf16[16,3584]{1,0:T(8,128)(2,1)S(1)}, u32[]{:S(2)}, u32[]{:S(2)}) collective-permute-start(bf16[16,3584]{1,0:T(8,128)(2,1)S(1)} %dynamic-slice_convert_fusion.2), channel_id=1, source_target_pairs={{0,8},{1,9},{2,10},{3,11},{4,12},{5,13},{6,14},{7,15},{8,0},{9,1},... | collective-permute-start | bytes 344072 | tf_op jit(solution)/shard_map/ppermute | solution.py:282
  241.1 2.2 copy-start.1
  243.3 132.5 %copy-start.2 = (f32[3584]{0:T(1024)S(1)}, f32[3584]{0:T(1024)}, u32[]{:S(2)}) copy-start(f32[3584]{0:T(1024)} %param.11) | copy-start | bytes 43012
  286.2 5.8 %collective-permute-start.4 = (bf16[8,3584]{1,0:T(8,128)(2,1)S(1)}, bf16[8,3584]{1,0:T(8,128)(2,1)S(1)}, u32[]{:S(2)}, u32[]{:S(2)}) collective-permute-start(bf16[8,3584]{1,0:T(8,128)(2,1)S(1)} %dynamic-slice_convert_fusion.3), channel_id=1, source_target_pairs={{0,16},{1,17},{2,18},{3,19},{4,20},{5,21},{6,22},{7,23},{8,24},{9,... | collective-permute-start | bytes 172040 | tf_op jit(solution)/shard_map/ppermute | solution.py:282
Sparse Core Ops, SparseCore 0:
  12.6 76.8 all-gather.5
  91.9 73.6 reduce-scatter.4
  167.3 73.7 all-gather.7
  243.4 132.3 reduce-scatter.2
where the time goes:
time: 474 us; the launch traced here: 473 us
  waiting for transfers between devices  178 us (38%)
  Pallas kernels  127 us (27%)
  matrix products  65.7 us (14%)
  blocking collectives  51.6 us (11%)
  other arithmetic  17.6 us (4%)
  between operations  16.4 us (3%)
  starting transfers between devices  8.47 us (2%)
  local copies, waits for them, and re-layouts  8.4 us (2%)
    reduce_scatter x1, waiting for transfers between devices, body(): upstream = lax.psum_scatter(upstream, 'dp', scatter_dimension=0, tiled=True)  83.8 us
    all_gather x2, waiting for transfers between devices, body(): lax.all_gather(a, 'dp', axis=0, tiled=True)  74.5 us
    pallas_call x1, Pallas kernels, reduce_hidden(): pl.pallas_call(functools.partial(hidden_kernel, levels, plans), out_shape...  71.6 us
    pallas_call x1, Pallas kernels, table_gradient(): pl.pallas_call(functools.partial(table_kernel, scale, step), grid=(row_co...  42.9 us
    all_gather x3, blocking collectives, body(): lax.all_gather(a, 'dp', axis=0, tiled=True)  26.2 us
    dot_general x1, matrix products, body(): lax.dot_general(table, normed_all, (((1,), (1,)), ((), ())), preferred_el...  23 us
    dot_general x1, matrix products, body(): lax.dot_general(slope, table, (((0,), (0,)), ((), ())), preferred_element...  22.3 us
    dot_general x1, matrix products, body(): lax.dot_general(id_hit, table, (((1,), (0,)), ((), ())), preferred_elemen...  20.4 us
  transfers between devices with their start and end apart: 9, of which 7 were waited for; matrix products, arithmetic and copies ran while one was open for 17% of the time, Pallas kernels for 12%

commit v1 on v0

v1 whole, which is shorter than its diff:
```python
import functools
import math

import jax
import jax.numpy as jnp
from jax import lax
from jax.experimental import pallas as pl
from jax.experimental.pallas import tpu as pltpu
from jax.sharding import PartitionSpec as P

SOFTCAP = 30
EPSILON = 1e-06
LANES = 128
F32, BF16, I16, I32 = jnp.float32, jnp.bfloat16, jnp.int16, jnp.int32

SIDE = 4
WIDE = 256
FULL = 32000.0
ORDERS = ((0, 2, 1), (2, 1, 0), (1, 0, 2))


def of(value, step):
    return value if isinstance(value, int) else pl.multiple_of(value, step)


def odd(j):
    return j % 2 if isinstance(j, int) else lax.rem(j, 2)


class Here:
    def __init__(self):
        self.y = lax.axis_index("dp")
        self.v = lax.axis_index("vocab")
        self.z = lax.div(self.v, 8)
        self.x = lax.rem(lax.div(self.v, 2), SIDE)
        self.c = lax.rem(self.v, 2)
        self.co = (self.y, self.z, self.x)
        self.near = [[p] + [lax.rem(p + s, SIDE) for s in (1, 2, 3)] for p in self.co]

    def peer(self, axis, step):
        if axis == 0:
            return {"dp": lax.rem(self.y + step, SIDE)}
        if axis == 1:
            return {"vocab": lax.rem(self.z + step, SIDE) * 8 + lax.rem(self.v, 8)}
        if axis == 2:
            return {"vocab": self.z * 8 + lax.rem(self.x + step, SIDE) * 2 + self.c}
        return {"vocab": self.v + 1 - 2 * self.c}

    def plus(self, axis, step):
        return self.near[axis][step]

    def enter(self, *groups):
        barrier = pltpu.get_barrier_semaphore()
        peers = [peer for group in groups for peer in group]
        for peer in peers:
            pl.semaphore_signal(barrier, inc=1, device_id=peer)
        pl.semaphore_wait(barrier, len(peers))

    def row(self):
        out = []
        for i in range(1, 8):
            x = self.near[2][i // 2]
            out.append({"vocab": self.z * 8 + x * 2 + (1 - self.c if i % 2 else self.c)})
        return out

    def face(self):
        out = []
        for i in range(1, 16):
            z = self.near[1][i % 4]
            out.append({"dp": self.near[0][i // 4], "vocab": z * 8 + lax.rem(self.v, 8)})
        return out

    def axes(self):
        return [self.peer(a, s) for a in range(3) for s in (1, 2, 3)]


class Lanes:
    def __init__(self, send, recv):
        self.send, self.recv, self.made = send, recv, []

    def go(self, ends):
        self.made.append(Trip(self, len(self.made), ends))
        return self.made[-1]


class Trip:
    def __init__(self, lanes, i, ends):
        self.lanes, self.i, self.ends, self.gone = lanes, i, ends, False

    def make(self):
        src, dst, device = self.ends()
        return pltpu.make_async_remote_copy(
            src_ref=src,
            dst_ref=dst,
            send_sem=self.lanes.send.at[self.i],
            recv_sem=self.lanes.recv.at[self.i],
            device_id=device,
        )

    def start(self):
        self.gone = True
        self.make().start()

    def wait_recv(self):
        self.make().wait_recv()

    def wait_send(self):
        self.make().wait_send()


class Scatter:
    def __init__(self, here, acc, slots, send, recv):
        self.here, self.acc, self.slots, self.send, self.recv = here, acc, slots, send, recv

    def index(self, j, o, stage, last):
        order = ORDERS[o]
        fixed = {order[k]: self.here.co[order[k]] for k in range(stage)}
        fixed[order[stage]] = last
        return (j,) + tuple(fixed.get(a, slice(None)) for a in range(3))

    def copies(self, j, o, stage):
        axis = ORDERS[o][stage]
        return [
            pltpu.make_async_remote_copy(
                src_ref=self.acc.at[self.index(j, o, stage, self.here.near[axis][i + 1])],
                dst_ref=self.slots[stage].at[j, i],
                send_sem=self.send.at[j, stage, i],
                recv_sem=self.recv.at[j, stage, i],
                device_id=self.here.peer(axis, i + 1),
            )
            for i in range(3)
        ]

    def step(self, k, j, o):
        if k > 0:
            for copy in self.copies(j, o, k - 1):
                copy.wait_recv()
            at = self.index(j, o, k - 1, self.here.co[ORDERS[o][k - 1]])
            got = self.slots[k - 1]
            self.acc[at] = (self.acc[at] + got[j, 0]) + (got[j, 1] + got[j, 2])
        if k < 3:
            for copy in self.copies(j, o, k):
                copy.start()

    def drain(self, j, o):
        for stage in range(3):
            for copy in self.copies(j, o, stage):
                copy.wait_send()


def scatter_scratch(tiles, dtype):
    dims = ((SIDE, SIDE), (SIDE,), ())
    slots = [pltpu.VMEM((tiles, 3, *d, 16, WIDE), dtype) for d in dims]
    sems = [pltpu.SemaphoreType.DMA((tiles, 3, 3))] * 2
    return [pltpu.VMEM((tiles, SIDE, SIDE, SIDE, 16, WIDE), dtype)] + slots + sems


class Spread:
    def __init__(self, here, lanes, buffer):
        self.here, self.lanes, self.buffer, self.flying = here, lanes, buffer, []
        self.width = buffer.shape[-1]

    def send(self, index, peer):
        return self.lanes.go(lambda: (self.buffer.at[index], self.buffer.at[index], peer()))

    def step(self, k):
        h, c = self.here, self.here.c
        for copy in self.flying:
            copy.wait_recv()
        every = slice(None)
        cut = self.width // WIDE // 2 * WIDE
        low, high = slice(0, cut), slice(cut, self.width)
        if k == 0:
            at = [((c, h.z, h.x, every, low), 2), ((c, h.z, h.x, every, high), 1)]
        elif k == 1:
            at = [((c, h.z, every, every, low), 1), ((c, every, h.x, every, high), 2)]
        else:
            at = []
        self.flying = [
            self.send(index, lambda axis=axis, s=s: h.peer(axis, s))
            for index, axis in at
            for s in (1, 3, 2)
        ]
        if k == 2:
            self.flying = [self.send((c,), lambda: h.peer(3, 1))]
        for copy in self.flying:
            copy.start()


class Gather:
    def __init__(self, here, lanes, block, shard, part):
        self.here, self.lanes, self.block, self.shard = here, lanes, block, shard
        y = here.y
        self.left, self.right, self.far = here.near[0][3], here.near[0][1], here.near[0][2]
        wide = 3 * WIDE
        lone = part - 2 * wide
        quarter, eighth, mid = shard // 4, shard // 8, shard // 2
        cuts = ((lone, 2), (lone + wide, 1))
        self.pieces, self.relays = [], []
        for column, axis in cuts:
            me = here.co[axis] * quarter
            self.pieces += self.pair(y, y, me, me, quarter, column, wide, 0)
            self.relays += self.pair(
                self.left, self.right, me, me + eighth, eighth, column, wide, 0
            )
        self.lone = self.pair(y, y, 0, 0, shard, 0, lone, 0)
        self.lone_relay = self.pair(self.left, self.right, 0, mid, mid, 0, lone, 0)
        self.around, self.passed = {}, {}
        for n, s in (("left", self.left), ("right", self.right), ("far", self.far)):
            self.around[n], self.passed[n] = [], []
            for column, axis in cuts:
                me = here.co[axis] * quarter
                down, up = here.near[axis][3] * quarter, here.near[axis][1] * quarter
                self.around[n] += self.pair(s, s, me, me, quarter, column, wide, axis)
                self.passed[n] += self.pair(s, s, down, up + eighth, eighth, column, wide, axis)

    def pair(self, s_up, s_down, at_up, at_down, count, column, size, axis):
        def trip(s, at, step):
            def ends():
                ref = lambda: self.block(s, at, count, column, size)
                return ref(), ref(), self.here.peer(axis, step)

            return self.lanes.go(ends)

        return [trip(s_up, at_up, 1), trip(s_down, at_down, 3)]


def start(copies):
    for copy in copies:
        copy.start()


def arrive(copies):
    for copy in copies:
        copy.wait_recv()


def forward_kernel(
    meta_ref, hidden_ref, gain_ref, cot_ref, table_ref,
    norm_out, cot_out, slope_out, slope_t_out, emb_ref, scale_out, loss_ref, meta_out,
    table, norm, tall, pre, slope, crecv, sbuf, meta, id_col, scale, mine, slot_r, slot_f,
    acc, slots0, slots1, slots2, tile_send, tile_recv,
    send_sem, recv_sem, core_send, core_recv, local_sem,
):
    here = Here()
    y, z, x, c = here.y, here.z, here.x, here.c
    rows, width = table_ref.shape
    part = width // 2
    shard = hidden_ref.shape[0]
    tokens = SIDE * shard
    tiles = part // WIDE
    padded = table.shape[1]
    first_row = (y * 32 + here.v) * rows
    lanes = Lanes(send_sem, recv_sem)
    scatter = Scatter(here, acc, (slots0, slots1, slots2), tile_send, tile_recv)

    loads = [
        pltpu.make_async_copy(
            table_ref.at[:, pl.ds(h * part, part)], table.at[h, pl.ds(0, rows)], local_sem.at[h]
        )
        for h in (0, 1)
    ]
    for load in loads:
        load.start()
    row, face = here.row(), here.face()
    row_at, face_at = x * 2 + c, y * SIDE + z
    here.enter(row, face)

    meta[y] = meta_ref[...]
    meta_copies = [
        lanes.go(lambda s=s: (meta_ref, meta.at[y], here.peer(0, s))) for s in (1, 2, 3)
    ]
    for copy in meta_copies:
        copy.start()

    own = of(y * shard, shard)

    def normalize(i, carry):
        at = pl.ds(of(i * 64, 64), 64)
        wide = hidden_ref[at, :].astype(F32)
        inv = lax.rsqrt(jnp.sum(wide * wide, axis=1, keepdims=True) / width + EPSILON)
        out = (wide * inv * gain_ref[...]).astype(BF16)
        to = pl.ds(of(own + i * 64, 64), 64)
        norm[0, to, :] = out[:, :part]
        norm[1, to, :] = out[:, part:]
        return carry

    lax.fori_loop(0, shard // 64, normalize, 0)

    def norm_block(s, offset, count, column, size):
        return norm.at[c, pl.ds(of(s * shard + offset, 16), count), pl.ds(column, size)]

    def cot_block(s, offset, count, column, size):
        at = pl.ds(of(s * shard + offset, 16), count)
        return cot_out.at[at, pl.ds(of(c * part + column, LANES), size)]

    normed = Gather(here, lanes, norm_block, shard, part)
    cots = Gather(here, lanes, cot_block, shard, part)
    across = {
        n: lanes.go(
            lambda s=s: (
                norm_block(s, 0, shard, 0, part), norm_block(s, 0, shard, 0, part), here.peer(3, 1)
            )
        )
        for n, s in (("left", normed.left), ("right", normed.right), ("far", normed.far))
    }
    start(normed.pieces)
    cot_local = pltpu.make_async_copy(cot_ref, cot_out.at[pl.ds(own, shard), :], local_sem.at[2])
    cot_local.start()

    for copy in meta_copies:
        copy.wait_recv()
    for s in range(SIDE):
        local = (meta[s, 0:1, :] - first_row).astype(F32)
        id_col[s * shard : (s + 1) * shard, :] = jnp.transpose(
            jnp.broadcast_to(local, (LANES, shard))
        ).astype(I32)

    def onehot(i, carry):
        at = pl.ds(of(i * 64, 64), 64)
        ids = id_col[at, :]
        lane = lax.broadcasted_iota(I32, (64, LANES), 1)
        for t in range(padded // LANES):
            inside = lane + t * LANES
            hit = ids == (jnp.where(inside < rows, inside, -1) if (t + 1) * LANES > rows else inside)
            tall[at, t * LANES : (t + 1) * LANES] = jnp.where(hit, 1.0, 0.0).astype(BF16)
        return carry

    lax.fori_loop(0, tokens // 64, onehot, 0)
    for h in (0, 1):
        table[h, rows:padded, :] = jnp.zeros((padded - rows, part), BF16)
    for load in loads:
        load.wait()

    def core_copy(j):
        return pltpu.make_async_remote_copy(
            src_ref=sbuf.at[odd(j)],
            dst_ref=crecv.at[j],
            send_sem=core_send.at[j],
            recv_sem=core_recv.at[j],
            device_id=here.peer(3, 1),
        )

    blocks = (SIDE, SIDE, SIDE, 16, WIDE)

    def find(j, carry):
        columns = pl.ds(of(j * WIDE, WIDE), WIDE)

        def product(h):
            out = jnp.dot(tall[...], table[h, :, columns], preferred_element_type=F32)
            return out.astype(BF16).reshape(blocks)

        @pl.when(j >= 2)
        def _():
            core_copy(j - 2).wait_send()

        other, mine_tile = product(1 - c), product(c)
        sbuf[odd(j)] = other
        acc[j] = mine_tile
        core_copy(j).start()

        @pl.when(j == 1)
        def _():
            arrive(normed.pieces)
            start(normed.relays + normed.around["left"] + normed.around["right"] + normed.lone)

        @pl.when(j == 3)
        def _():
            arrive(normed.relays)
            start(normed.around["far"])

        @pl.when(j == 4)
        def _():
            arrive(normed.around["left"] + normed.around["right"])
            start(normed.passed["left"] + normed.passed["right"])
            arrive(normed.lone)
            start(normed.lone_relay)

        @pl.when(j == 5)
        def _():
            arrive(normed.around["far"])
            start(normed.passed["far"])
            cot_local.wait()
            start(cots.pieces)

        @pl.when(j == 6)
        def _():
            arrive(normed.passed["left"] + normed.passed["right"])
            start([across["left"], across["right"]])

        return carry

    lax.fori_loop(0, tiles, find, 0)
    arrive(normed.lone_relay + normed.passed["far"])
    across["far"].start()
    for j in range(tiles):
        core_copy(j).wait_recv()
        acc[j] = acc[j] + crecv[j]
        scatter.step(0, j, j % 3)
    arrive(list(across.values()))
    norm_copies = [
        pltpu.make_async_copy(norm.at[h], norm_out.at[h], local_sem.at[3 + h]) for h in (0, 1)
    ]
    for copy in norm_copies:
        copy.start()

    group = 2 * shard
    tall_rows = rows // 5
    def target_of(g):
        both_rows = [meta[2 * g + i, 1:2, :] - first_row for i in (0, 1)]
        row = jnp.concatenate(both_rows, axis=1)
        return jnp.where((row >= 0) & (row < rows), row, -1)

    def weight_of(g):
        return jnp.concatenate([meta[2 * g + i, 2:3, :] for i in (0, 1)], axis=1).astype(F32)

    def found_step(k):
        for j in range(tiles):
            scatter.step(k, j, j % 3)

    def emit():
        for j in range(tiles):
            found = acc[j, y, z, x].astype(F32) * math.sqrt(width)
            emb_ref[:, j * WIDE : (j + 1) * WIDE] = found.astype(BF16)

    def cot_start():
        arrive(cots.pieces)
        start(cots.relays + cots.around["left"] + cots.around["right"] + cots.lone)

    def cot_far():
        arrive(cots.relays)
        start(cots.around["far"])

    def cot_pass():
        arrive(cots.around["left"] + cots.around["right"] + cots.lone)
        start(cots.passed["left"] + cots.passed["right"] + cots.lone_relay)

    def cot_last():
        arrive(cots.around["far"])
        start(cots.passed["far"])

    plan = {0: cot_start, 2: cot_far, 4: cot_pass, 5: lambda: found_step(1), 6: cot_last,
            7: lambda: found_step(2)}

    def exchange_start(g, stage):
        me, slots = ((row_at, slot_r), (face_at, slot_f))[stage]
        peers = (row, face)[stage]
        slots[g, me] = mine[g, stage]
        out = [
            lanes.go(lambda p=p: (mine.at[g, stage], slots.at[g, me], p)) for p in peers
        ]
        start(out)
        return out

    def exchange_step(g, stage, flying):
        arrive(flying)
        slots = (slot_r, slot_f)[stage - 1]
        parts = [slots[g, i] for i in range(slots.shape[1])]
        while len(parts) > 1:
            parts = [a + b for a, b in zip(parts[::2], parts[1::2])]
        mine[g, stage] = parts[0]
        return exchange_start(g, stage) if stage < 2 else []

    flights = {}
    for g in (0, 1):
        target = target_of(g)
        token_at = slice(g * group, (g + 1) * group)

        def logits(r, carry, g=g, target=target, token_at=token_at):
            at = pl.ds(of(r * tall_rows, 16), tall_rows)
            raw = [
                lax.dot_general(
                    table[h, at, :], norm[h, token_at, :],
                    (((1,), (1,)), ((), ())), preferred_element_type=F32,
                )
                for h in (0, 1)
            ]
            pre[at, token_at] = raw[0] + raw[1]

            def shape(i, sums):
                total, picked = sums
                rows_at = pl.ds(of(r * tall_rows + i * 40, 8), 40)
                bent = jnp.tanh(pre[rows_at, token_at] * (1.0 / SOFTCAP))
                grown = jnp.exp(bent * SOFTCAP)
                pre[rows_at, token_at] = grown * (1.0 - bent * bent)
                ids = lax.broadcasted_iota(I32, bent.shape, 0) + (r * tall_rows + i * 40)
                found = jnp.where(ids == target, bent, 0.0)
                fold = lambda a: jnp.sum(a.reshape(5, 8, group), axis=0)
                return total + fold(grown), picked + fold(found)

            carry = lax.fori_loop(0, tall_rows // 40, shape, carry)
            for i in range(5):
                k = 5 * g + i
                if k in plan:

                    @pl.when(r == i)
                    def _(k=k):
                        plan[k]()

            if g == 1:
                for i in (1, 2):

                    @pl.when(r == 2 * i - 1)
                    def _(i=i):
                        flights[0] = exchange_step(0, i, flights[0])

            return carry

        zero = jnp.zeros((8, group), F32)
        total, picked = lax.fori_loop(0, 5, logits, (zero, zero))
        total = jnp.sum(total, axis=0, keepdims=True)
        picked = jnp.sum(picked, axis=0, keepdims=True)
        for i in range(group // LANES):
            mine[g, 0, i : i + 1, :] = total[:, i * LANES : (i + 1) * LANES]
            mine[g, 0, 4 + i : 5 + i, :] = picked[:, i * LANES : (i + 1) * LANES]
        flights[g] = exchange_start(g, 0)

    pre[rows:padded, :] = jnp.zeros((padded - rows, tokens), F32)
    sums = []

    def slopes(g):
        target, weight = target_of(g), weight_of(g)
        stats = mine[g, 2]
        lines = [jnp.concatenate([stats[i + 4 * k : i + 4 * k + 1] for i in range(4)], axis=1) for k in (0, 1)]
        total, bent = lines
        chosen = jnp.exp(bent * SOFTCAP) / total
        sums.append(
            (
                jnp.sum(weight * (jnp.log(total) - SOFTCAP * bent), axis=1, keepdims=True),
                jnp.sum(weight, axis=1, keepdims=True),
            )
        )
        bound = 0.17 * (jnp.maximum(1.0 - chosen, 0.0) + 1e-5)
        scale[g * group : (g + 1) * group, :] = jnp.transpose(
            jnp.broadcast_to(bound, (LANES, group))
        )
        factor = weight / total
        drop = weight * (1.0 - bent * bent)

        def turn(i, carry):
            at = pl.ds(of(i * WIDE, WIDE), WIDE)
            ids = lax.broadcasted_iota(I32, (WIDE, shard), 0) + i * WIDE
            for s in (0, 1):
                here_at = slice(g * group + s * shard, g * group + (s + 1) * shard)
                cut = slice(s * shard, (s + 1) * shard)
                value = pre[at, here_at] * factor[:, cut]
                value = value - jnp.where(ids == target[:, cut], drop[:, cut], 0.0)
                low = value.astype(BF16)
                slope[at, here_at] = low
                tall[here_at, at] = jnp.transpose(low)
            return carry

        lax.fori_loop(0, padded // WIDE, turn, 0)
        copies = []
        for k, (src, dst) in enumerate(
            ((slope.at[:, g * group : (g + 1) * group], slope_out.at[:, g * group : (g + 1) * group]),
             (tall.at[g * group : (g + 1) * group], slope_t_out.at[g * group : (g + 1) * group]))
        ):
            copies.append(pltpu.make_async_copy(src, dst, local_sem.at[5 + 2 * g + k]))
            copies[-1].start()
        return copies

    found_step(3)
    emit()
    flights[1] = exchange_step(1, 1, flights[1])
    out_copies = slopes(0)
    flights[1] = exchange_step(1, 2, flights[1])
    out_copies += slopes(1)
    loss = (sums[0][0] + sums[1][0]) / jnp.maximum(sums[0][1] + sums[1][1], 1.0)
    loss_ref[...] = jnp.broadcast_to(loss, loss_ref.shape)
    meta_out[...] = meta[...]
    scale_copy = pltpu.make_async_copy(scale, scale_out, local_sem.at[9])
    scale_copy.start()
    arrive(cots.passed["left"] + cots.passed["right"] + cots.passed["far"] + cots.lone_relay)
    for copy in out_copies + [scale_copy] + norm_copies:
        copy.wait()
    for copy in lanes.made:
        if copy.gone:
            copy.wait_send()
    for j in range(tiles):
        if j >= tiles - 2:
            core_copy(j).wait_send()
        scatter.drain(j, j % 3)


def backward_kernel(
    slope_t_ref, scale_ref, ids_ref, emb_ref, hidden_ref, gain_ref, slope_ref, norm_ref, cot_ref, table_ref,
    grad_out, emb_out, gain_out, head_out, cot_other,
    table, norm, slope, hit, crecv, sbuf, held, grad, emb, cots, wide, up, dots, gains, slot_g, slot_c,
    acc, slots0, slots1, slots2, tile_send, tile_recv,
    send_sem, recv_sem, core_send, core_recv, local_sem, cot_sem, out_sem,
):
    here = Here()
    y, z, x, c = here.y, here.z, here.x, here.c
    rows, width = table_ref.shape
    part = width // 2
    tiles = part // WIDE
    padded = table.shape[1]
    tokens = slope_t_ref.shape[0]
    shard = tokens // SIDE
    lanes = Lanes(send_sem, recv_sem)
    scatter = Scatter(here, acc, (slots0, slots1, slots2), tile_send, tile_recv)
    blocks = (SIDE, SIDE, SIDE, 16, WIDE)
    first_row = (y * 32 + here.v) * rows

    def load(h):
        return pltpu.make_async_copy(
            table_ref.at[:, pl.ds(of(h * part, LANES), part)],
            table.at[h, pl.ds(0, rows)],
            local_sem.at[4 + h],
        )

    load(1 - c).start()
    load(c).start()
    mine_at = (z * SIDE + x) * 16
    row_loads = [
        pltpu.make_async_copy(
            hidden_ref.at[pl.ds(of(mine_at, 16), 16), pl.ds(h * part, part)],
            wide.at[h],
            local_sem.at[h],
        )
        for h in (0, 1)
    ]
    later = [
        pltpu.make_async_copy(slope_ref, slope, local_sem.at[6]),
        pltpu.make_async_copy(norm_ref, norm, local_sem.at[7]),
    ]
    for copy in row_loads + later:
        copy.start()
    here.enter(here.axes(), [here.peer(3, 1)])
    cot_across = lanes.go(
        lambda: (
            cot_ref.at[:, pl.ds(of(c * part, LANES), part)], cot_other, here.peer(3, 1)
        )
    )
    emb[c, z, x] = emb_ref[...]
    emb_spread, spread = Spread(here, lanes, emb), Spread(here, lanes, grad)
    emb_spread.step(0)
    for h in (0, 1):
        table[h, rows:padded, :] = jnp.zeros((padded - rows, part), BF16)

    def match(i, carry):
        at = pl.ds(of(i * 80, 16), 80)
        ids = lax.broadcasted_iota(I32, (80, shard), 0) + (first_row + i * 80)
        for s in range(SIDE):
            found = jnp.where(ids == ids_ref[s, 0:1, :], 1.0, 0.0)
            hit[at, s * shard : (s + 1) * shard] = found.astype(BF16)
        return carry

    lax.fori_loop(0, rows // 80, match, 0)

    def core_copy(j):
        return pltpu.make_async_remote_copy(
            src_ref=sbuf.at[odd(j)],
            dst_ref=crecv.at[j],
            send_sem=core_send.at[j],
            recv_sem=core_recv.at[j],
            device_id=here.peer(3, 1),
        )

    delays = (1, 5, 7, 9)

    def substeps(s):
        for k in range(4):
            j = s - delays[k]

            @pl.when((j >= 0) & (j < tiles))
            def _(k=k, j=j):
                if k == 0:
                    core_copy(j).wait_recv()

                    def fit(i, carry):
                        at = pl.ds(of(i * shard, shard), shard)
                        factor = FULL / scale_ref[at, :]
                        total = held[odd(j), at, :] + crecv[j, at, :]
                        total = total * jnp.concatenate([factor] * (WIDE // LANES), axis=1)
                        whole = jnp.round(total).astype(I32).astype(I16)
                        acc[j, i] = whole.reshape(blocks[1:])
                        return carry

                    lax.fori_loop(0, SIDE, fit, 0)
                for o in range(3):

                    @pl.when(lax.rem(j, 3) == o)
                    def _(o=o):
                        scatter.step(k, j, o)

    def tile(j, carry):
        columns = pl.ds(of(j * WIDE, WIDE), WIDE)

        def product(h):
            return jnp.dot(slope_t_ref[...], table[h, :, columns], preferred_element_type=F32)

        @pl.when(j >= 2)
        def _():
            core_copy(j - 2).wait_send()

        other, mine_tile = product(1 - c), product(c)
        sbuf[odd(j)] = other
        held[odd(j)] = mine_tile
        core_copy(j).start()
        substeps(j)
        for i, k in ((2, 1), (5, 2)):

            @pl.when(j == i)
            def _(k=k):
                emb_spread.step(k)

        return carry

    load(1 - c).wait()
    load(c).wait()
    lax.fori_loop(0, tiles, tile, 0)
    cot_across.start()
    for copy in row_loads + later:
        copy.wait()

    def cot_loads(g):
        j = lax.rem(g, tiles)
        mine_half = cot_ref.at[:, pl.ds(of(c * part + j * WIDE, LANES), WIDE)]
        other_half = cot_other.at[:, pl.ds(of(j * WIDE, LANES), WIDE)]
        return [
            pltpu.make_async_copy(half, cots.at[odd(g)], cot_sem.at[odd(g)])
            for half in (mine_half, other_half)
        ]

    def cot_start(g):
        @pl.when(g < tiles)
        def _():
            cot_loads(g)[0].start()

        @pl.when(g >= tiles)
        def _():
            cot_loads(g)[1].start()

    def head_copy(g):
        j = lax.rem(g, tiles)
        h = jnp.where(g < tiles, c, 1 - c)
        return pltpu.make_async_copy(
            table.at[h, pl.ds(0, rows), pl.ds(of(j * WIDE, WIDE), WIDE)],
            head_out.at[:, pl.ds(of(h * part + j * WIDE, LANES), WIDE)],
            out_sem.at[g],
        )

    flying = {}

    def gain_send(stage):
        axis = (2, 1, 0)[stage]
        slot_g[stage, here.co[axis]] = gains[stage]
        out = [
            lanes.go(
                lambda s=s: (gains.at[stage], slot_g.at[stage, here.co[axis]], here.peer(axis, s))
            )
            for s in (1, 2, 3)
        ]
        start(out)
        flying["gain"] = out

    def gain_sum(stage):
        arrive(flying["gain"])
        slots = [slot_g[stage, i] for i in range(SIDE)]
        gains[stage + 1] = (slots[0] + slots[1]) + (slots[2] + slots[3])

    def pieces():
        both = [wide[h].astype(F32) for h in (0, 1)]
        square = sum(jnp.sum(b * b, axis=1, keepdims=True) for b in both) / width
        return lax.rsqrt(square + EPSILON), wide[c].astype(F32)

    def finish():
        unit = scale_ref[pl.ds(of(y * shard + mine_at, 16), 16), 0:1] * (1.0 / FULL)
        for j in range(tiles):
            up[:, j * WIDE : (j + 1) * WIDE] = acc[j, y, z, x].astype(I32).astype(F32) * unit
        inv, ours = pieces()
        dot = jnp.sum(up[...] * gain_ref[c] * ours, axis=1, keepdims=True)
        dots[0] = jnp.broadcast_to(dot, (16, LANES))
        slot_c[c] = dots[0]
        flying["dot"] = [lanes.go(lambda: (dots.at[0], slot_c.at[c], here.peer(3, 1)))]
        start(flying["dot"])
        gain_part = jnp.sum(up[...] * ours * inv, axis=0, keepdims=True)
        for j in range(part // LANES):
            gains[0, j : j + 1, :] = gain_part[:, j * LANES : (j + 1) * LANES]
        lines = gains.shape[1]
        gains[0, part // LANES : lines, :] = jnp.zeros((lines - part // LANES, LANES), F32)
        gain_send(0)

    def gradient():
        arrive(flying["dot"])
        inv, ours = pieces()
        mean_dot = (slot_c[0, :, 0:1] + slot_c[1, :, 0:1]) / width
        out = inv * (up[...] * gain_ref[c]) - ours * (inv * inv * inv) * mean_dot
        grad[c, z, x] = out.astype(BF16)
        spread.step(0)

    def gain_last():
        gain_sum(2)
        gain_out[c] = gains[3]
        slot_g[3, c] = gains[3]
        flying["gain"] = [lanes.go(lambda: (gains.at[3], slot_g.at[3, c], here.peer(3, 1)))]
        start(flying["gain"])

    def wide_out(buffer, out, at):
        return [
            pltpu.make_async_copy(
                buffer.at[h], out.at[:, :, :, pl.ds(h * part, part)], local_sem.at[at + h]
            )
            for h in (0, 1)
        ]

    plan = {
        3: lambda: (arrive(emb_spread.flying), [o.start() for o in wide_out(emb, emb_out, 2)]),
        5: lambda: arrive([cot_across]),
        8: finish,
        9: lambda: (gradient(), gain_sum(0), gain_send(1)),
        11: lambda: (spread.step(1), gain_sum(1), gain_send(2)),
        13: lambda: (spread.step(2), gain_last()),
    }
    cot_start(0)

    def head(g, carry):
        j = lax.rem(g, tiles)
        h = jnp.where(g < tiles, c, 1 - c)
        columns = pl.ds(of(j * WIDE, WIDE), WIDE)

        @pl.when(g + 1 < 2 * tiles)
        def _():
            cot_start(g + 1)

        cot_loads(g)[0].wait()
        first = jnp.dot(slope[0:rows, :], norm[h, :, columns], preferred_element_type=F32)
        second = jnp.dot(hit[...], cots[odd(g)], preferred_element_type=F32)
        table[h, 0:rows, columns] = (first + second * math.sqrt(width)).astype(BF16)
        head_copy(g).start()
        substeps(g + tiles)
        for i in plan:

            @pl.when(g == i)
            def _(i=i):
                plan[i]()

        return carry

    lax.fori_loop(0, 2 * tiles, head, 0)
    arrive(spread.flying)
    outs = wide_out(grad, grad_out, 0)
    for copy in outs:
        copy.start()
    arrive(flying["gain"])
    gain_out[1 - c] = slot_g[3, 1 - c]
    for copy in outs + wide_out(emb, emb_out, 2):
        copy.wait()

    def heads_done(g, carry):
        head_copy(g).wait()
        return carry

    lax.fori_loop(0, 2 * tiles, heads_done, 0)
    for copy in lanes.made:
        if copy.gone:
            copy.wait_send()
    for j in range(tiles):
        if j >= tiles - 2:
            core_copy(j).wait_send()
        scatter.drain(j, j % 3)


def body(input_ids, target_ids, loss_mask, final_hidden, norm_gain, embed_cotangent, table):
    rows, width = table.shape
    shard = final_hidden.shape[0]
    tokens, part = SIDE * shard, width // 2
    tiles = part // WIDE
    padded = -(-rows // WIDE) * WIDE
    group = 2 * shard
    first_row = lax.axis_index(("dp", "vocab")) * rows
    meta = jnp.pad(jnp.stack([input_ids, target_ids, loss_mask]), ((0, 5), (0, 0)))
    any_ = pl.BlockSpec(memory_space=pl.ANY)
    vmem = pl.BlockSpec(memory_space=pltpu.VMEM)
    dma = pltpu.SemaphoreType.DMA
    share = (SIDE, SIDE, 16)
    blocks = (SIDE, SIDE, SIDE, 16, WIDE)
    norm_all, cot_all, slope, slope_t, found, bound, loss, meta_all = pl.pallas_call(
        forward_kernel,
        out_shape=(
            jax.ShapeDtypeStruct((2, tokens, part), BF16),
            jax.ShapeDtypeStruct((tokens, width), BF16),
            jax.ShapeDtypeStruct((padded, tokens), BF16),
            jax.ShapeDtypeStruct((tokens, padded), BF16),
            jax.ShapeDtypeStruct((16, part), BF16),
            jax.ShapeDtypeStruct((tokens, LANES), F32),
            jax.ShapeDtypeStruct((8, LANES), F32),
            jax.ShapeDtypeStruct((SIDE, 8, shard), I32),
        ),
        in_specs=[vmem, vmem, vmem, vmem, any_],
        out_specs=(any_, any_, any_, any_, vmem, any_, vmem, vmem),
        scratch_shapes=[
            pltpu.VMEM((2, padded, part), BF16),
            pltpu.VMEM((2, tokens, part), BF16),
            pltpu.VMEM((tokens, padded), BF16),
            pltpu.VMEM((padded, tokens), F32),
            pltpu.VMEM((padded, tokens), BF16),
            pltpu.VMEM((tiles, *blocks), BF16),
            pltpu.VMEM((2, *blocks), BF16),
            pltpu.VMEM((SIDE, 8, shard), I32),
            pltpu.VMEM((tokens, LANES), I32),
            pltpu.VMEM((tokens, LANES), F32),
            pltpu.VMEM((2, 3, 8, LANES), F32),
            pltpu.VMEM((2, 8, 8, LANES), F32),
            pltpu.VMEM((2, 16, 8, LANES), F32),
            *scatter_scratch(tiles, BF16),
            dma((140,)), dma((140,)), dma((tiles,)), dma((tiles,)), dma((12,)),
        ],
        compiler_params=pltpu.CompilerParams(
            collective_id=1, has_side_effects=True, vmem_limit_bytes=62 * 1024 * 1024
        ),
    )(meta, final_hidden, norm_gain.reshape(1, width), embed_cotangent, table)
    grad, embedded, gain, head, _ = pl.pallas_call(
        backward_kernel,
        out_shape=(
            jax.ShapeDtypeStruct((*share, width), BF16),
            jax.ShapeDtypeStruct((*share, width), BF16),
            jax.ShapeDtypeStruct((2, 16, LANES), F32),
            jax.ShapeDtypeStruct((rows, width), BF16),
            jax.ShapeDtypeStruct((tokens, part), BF16),
        ),
        in_specs=[vmem, vmem, vmem, vmem, any_, vmem, any_, any_, any_, any_],
        out_specs=(any_, any_, vmem, any_, any_),
        scratch_shapes=[
            pltpu.VMEM((2, padded, part), BF16),
            pltpu.VMEM((2, tokens, part), BF16),
            pltpu.VMEM((padded, tokens), BF16),
            pltpu.VMEM((rows, tokens), BF16),
            pltpu.VMEM((tiles, tokens, WIDE), F32),
            pltpu.VMEM((2, tokens, WIDE), F32),
            pltpu.VMEM((2, tokens, WIDE), F32),
            pltpu.VMEM((2, *share, part), BF16),
            pltpu.VMEM((2, *share, part), BF16),
            pltpu.VMEM((2, tokens, WIDE), BF16),
            pltpu.VMEM((2, 16, part), BF16),
            pltpu.VMEM((16, part), F32),
            pltpu.VMEM((1, 16, LANES), F32),
            pltpu.VMEM((4, 16, LANES), F32),
            pltpu.VMEM((4, SIDE, 16, LANES), F32),
            pltpu.VMEM((2, 16, LANES), F32),
            *scatter_scratch(tiles, I16),
            dma((50,)), dma((50,)), dma((tiles,)), dma((tiles,)), dma((8,)), dma((2,)),
            dma((2 * tiles,)),
        ],
        compiler_params=pltpu.CompilerParams(
            collective_id=2, has_side_effects=True, vmem_limit_bytes=63 * 1024 * 1024
        ),
    )(
        slope_t, bound, meta_all, found, final_hidden, norm_gain.reshape(2, 1, part),
        slope, norm_all, cot_all, table,
    )
    gain_grad = gain[:, : part // LANES, :].reshape(width)
    return (
        embedded.reshape(shard, width),
        loss[0, 0],
        grad.reshape(shard, width),
        gain_grad,
        head,
    )


def solution(mesh):
    placed = (
        P("dp"),
        P("dp"),
        P("dp"),
        P("dp", None),
        P(),
        P("dp", None),
        P(("dp", "vocab"), None),
    )
    return jax.shard_map(
        body,
        mesh=mesh,
        in_specs=placed,
        out_specs=(P("dp", None), P(), P("dp", None), P(), P(("dp", "vocab"), None)),
        check_vma=False,
    )
```

time: 474 us -> 197 us (0.42)
  waiting for transfers between devices: 178 us -> 0 us
  matrix products: 65.7 us -> 0 us
  blocking collectives: 51.6 us -> 0 us
  Pallas kernels: 127 us -> 169 us
  other arithmetic: 17.6 us -> 0.72 us
  between operations: 16.4 us -> 0.66 us
  local copies, waits for them, and re-layouts: 8.4 us -> 22.9 us
  starting transfers between devices: 8.47 us -> 0 us
    reduce_scatter x2 -> x0, waiting for transfers between devices: 83.8 us -> none  [the longest x1 83.8 us: body(): upstream = lax.psum_scatter(upstream, 'dp', scatter_dimension=0, tiled=True)]
    all_gather x2 -> x0, waiting for transfers between devices: 74.5 us -> none  [body(): lax.all_gather(a, 'dp', axis=0, tiled=True)]
    dot_general x3 -> x0, matrix products: 65.7 us -> none  [the longest x1 23 us: body(): lax.dot_general(table, normed_all, (((1,), (1,)), ((), ())), preferred_el...]
    pallas_call x3 -> x2, Pallas kernels: 127 us -> 169 us  [the longest x1 89 us: body(): pl.pallas_call(forward_kernel, out_shape=(jax.ShapeDtypeStruct((2, tokens...]
    all_gather x3 -> x0, blocking collectives: 26.2 us -> none  [body(): lax.all_gather(a, 'dp', axis=0, tiled=True)]
    psum x2 -> x0, blocking collectives: 25.4 us -> none  [the longest x1 15.6 us: body(): gain_grad = lax.psum(gain_part, 'dp')]
    ppermute x5 -> x0, waiting for transfers between devices: 19.2 us -> none  [halving_sum(): arrived = lax.ppermute(give.astype(jnp.bfloat16), 'vocab', pairs)]
    convert_element_type x6 -> x0, other arithmetic: 12.8 us -> none  [the longest x1 6.43 us: body(): slope = (token_weight[None, :] * (jnp.exp(capped) / sum_exp[None, :] - ta...]
  transfers between devices with their start and end apart: 9 -> 0, of which waited for: 7 -> 0; matrix products, arithmetic and copies ran while one was open for 17% -> 0% of each run, Pallas kernels for 12% -> 0%
where the time goes in v1:
time: 197 us; the launch traced here: 194 us
  Pallas kernels  169 us (86%)
  local copies, waits for them, and re-layouts  22.9 us (12%)
    pallas_call x1, Pallas kernels, body(): pl.pallas_call(forward_kernel, out_shape=(jax.ShapeDtypeStruct((2, tokens...  89 us
    pallas_call x1, Pallas kernels, body(): pl.pallas_call(backward_kernel, out_shape=(jax.ShapeDtypeStruct((*share,...  80.3 us
    unnamed x5, local copies, waits for them, and re-layouts  17 us

profile of v1, /device:TPU:0, one launch (start us, length us, event | category | flops | bytes accessed | tf_op | source)
XLA Modules:
  0.0 193.5 jit_solution(15760331150754226266)
XLA Ops:
  0.6 0.7 pad_add_fusion
  1.4 0.6 pad.4.meta_ref
  2.0 1.3 reshape.26.gain_ref
  3.3 1.3 reshape.25.gain_ref
  4.6 89.0 %shard_map.110 = (bf16[2,1024,1792]{2,1,0:T(8,128)(2,1)}, bf16[1024,3584]{1,0:T(8,128)(2,1)}, bf16[2048,1024]{1,0:T(8,128)(2,1)}, bf16[1024,2048]{1,0:T(8,128)(2...) custom-call(s32[8,256]{1,0:T(8,128)} %pad.4.meta_ref, ...), custom_call_target="tpu_custom_call" | custom-call | tf_op jit(solution)/shard_map/pallas_call | solution.py:880
  93.6 1.2 slice.6
  94.8 80.3 %shard_map.111 = (bf16[4,4,16,3584]{3,2,1,0:T(8,128)(2,1)}, bf16[4,4,16,3584]{3,2,1,0:T(8,128)(2,1)}, f32[2,16,128]{2,1,0:T(8,128)}, bf16[2000,3584]{1,0:T(8,128)(2,1)}, bf16[1024,1792]{1,0:T(8,128)(2,1)}) custom-call(bf16[1024,2048]{1,0:T(8,128)(2,1)} %get-tuple-element.17.slope_t_ref, f32[1024,128]{1,0:T(8,128)} %get-tuple-element.18.scale_ref, ...), custom_call_target="tpu_custom_call" | custom-call | tf_op jit(solution)/shard_map/pallas_call | solution.py:915
  175.1 0.0 copy-start
  175.1 1.5 reshape.29
  176.5 2.8 %copy.15 = bf16[256,3584]{1,0:T(8,128)(2,1)} copy(bf16[256,3584]{1,0:T(8,128)(2,1)} %bitcast.8) | data formatting | bytes 3670016
  179.4 0.0 copy-done
  179.4 1.2 copy.16
  180.6 12.9 %copy.17 = bf16[2000,3584]{1,0:T(8,128)(2,1)} copy(bf16[2000,3584]{1,0:T(8,128)(2,1)} %get-tuple-element.38) | data formatting | bytes 28672000
Async XLA Ops:
  175.1 4.3 %copy-start = (bf16[4,4,16,3584]{3,2,1,0:T(8,128)(2,1)S(1)}, bf16[4,4,16,3584]{3,2,1,0:T(8,128)(2,1)}, u32[]{:S(2)}) copy-start(bf16[4,4,16,3584]{3,2,1,0:T(8,128)(2,1)} %get-tuple-element.26) | copy-start | bytes 5505028
